TPU v7x, 256 devices: a whole 4x4x8 slice. The times are simulated.
256 devices in a mesh: dp: 64 (over y, z, core), mp: 4 (over x).
Axes of the slice: x: 4, y: 4, z: 8, core: 2. Of those that a mesh axis runs over, the one named last changes fastest.
Arguments:
- queries: bfloat16 [32768, 4096], P('dp', 'mp'), may hold values from -6 to 6
- passages: bfloat16 [32768, 4096], P('dp', 'mp'), may hold values from -6 to 6
- labels: int32 [32768], P('dp'), may hold values from 0 to 32767
- projection: bfloat16 [4096, 128], P('mp'), may hold values from -0.09375 to 0.09375
Outputs:
- loss: float32 [32768], P('dp')
- query_embed: bfloat16 [32768, 128], P('dp')
All inputs are finite; a program needn't handle non-finite values.
Results may differ from a plain program's by a relative error of at most 0.0039.
Values may be sent and summed in bfloat16 or wider, within the bound.
A program may use at most 64 MiB of HBM per device.

v0:
```python
import jax
import jax.numpy as jnp
from jax import lax
from jax.sharding import PartitionSpec as P


def copy_for_each(array, axis):
    devices = lax.axis_size(axis)
    return lax.all_to_all(
        jnp.broadcast_to(array[None], (devices, *array.shape)), axis, 0, 0, tiled=True
    )


def of_everyone(array, axis):
    everything = copy_for_each(array, axis)
    return jnp.sum(everything, axis=0)


def cut_along(array, dim, devices):
    before, after = (array.shape[:dim], array.shape[dim + 1 :])
    return jnp.moveaxis(array.reshape(*before, devices, -1, *after), dim, 0)


def summed_on_arrival(array, axis, dim):
    devices = lax.axis_size(axis)
    pieces = lax.all_to_all(cut_along(array, dim, devices), axis, 0, 0, tiled=True)
    return jnp.sum(pieces.astype(jnp.float32), axis=0)


def laid_out(pieces, dim):
    dims = list(pieces.shape[1:])
    dims[dim] *= pieces.shape[0]
    return jnp.moveaxis(pieces, 0, dim).reshape(dims)


def gathered_copies(array, axis, dim):
    return laid_out(copy_for_each(array, axis), dim)


def all_in_one(array, axis):
    leaves = jax.tree.leaves(array)
    order = sorted(range(len(leaves)), key=lambda k: -leaves[k].size)
    width = (1, *leaves[order[0]].shape)[-1]
    lines = [
        jnp.pad(leaves[k].reshape(-1), (0, -leaves[k].size % width)).reshape(-1, width)
        for k in order
    ]
    both, at, found = (copy_for_each(jnp.concatenate(lines), axis), 0, {})
    for k, line in zip(order, lines):
        section = both[:, at : at + len(line)].reshape(len(both), -1)
        found[k] = section[:, : leaves[k].size].reshape(-1, *leaves[k].shape)
        at += len(line)
    numbers = iter(range(len(leaves)))
    return jax.tree.map(lambda _: found[next(numbers)], array)


def combined_pairwise(pieces, combine):
    while len(jax.tree.leaves(pieces)[0]) > 1:
        pieces = jax.vmap(combine)(
            *(jax.tree.map(lambda part: part[side::2], pieces) for side in (0, 1))
        )
    return jax.tree.map(lambda part: part[0], pieces)


def combined_all(array, axis, combine):
    pieces = all_in_one(array, axis)
    return combined_pairwise(pieces, combine)


def combine_stats(first, second):
    top = jnp.maximum(first[0], second[0])
    total = first[1] * jnp.exp(first[0] - top) + second[1] * jnp.exp(second[0] - top)
    return (top, total, first[2] + second[2])


def block_columns(count):
    target = 2048
    best = 1
    for option in range(1, target + 1):
        if count % option == 0:
            best = option
    return best


def per_device(queries, passages, labels, projection):
    query_part = jnp.dot(queries, projection, preferred_element_type=jnp.float32)
    passage_part = jnp.dot(passages, projection, preferred_element_type=jnp.float32)
    rows = query_part.shape[0]
    embed = query_part.shape[1]
    query_embed = of_everyone(query_part, "mp").astype(jnp.bfloat16)
    passage_embed = summed_on_arrival(passage_part.astype(jnp.bfloat16), "mp", 0).astype(
        jnp.bfloat16
    )
    offset = lax.axis_index("mp") * passage_embed.shape[0]
    width = passage_embed.shape[0]
    start_state = (
        jnp.full((rows,), -jnp.inf, jnp.float32),
        jnp.zeros((rows,), jnp.float32),
        jnp.zeros((rows,), jnp.float32),
    )
    piece = gathered_copies(passage_embed, "dp", 0)
    count = piece.shape[0]
    columns_each = block_columns(count)
    blocks = piece.reshape(count // columns_each, columns_each, embed)
    firsts = jnp.arange(blocks.shape[0], dtype=jnp.int32) * columns_each

    def step(state, item):
        block, first = item
        scores = lax.dot_general(
            query_embed, block, (((1,), (1,)), ((), ())), preferred_element_type=jnp.float32
        )
        columns = first + lax.iota(jnp.int32, columns_each)
        passage_ids = columns // width * rows + offset + columns % width
        hit = passage_ids[None, :] == labels[:, None]
        chosen = jnp.sum(jnp.where(hit, scores, 0.0), axis=1)
        block_top = jnp.max(scores, axis=1)
        block_sum = jnp.sum(jnp.exp(scores - block_top[:, None]), axis=1)
        return (combine_stats(state, (block_top, block_sum, chosen)), None)

    result, unused = lax.scan(step, start_state, (blocks, firsts))
    top, total, chosen = combined_all(result, "mp", combine_stats)
    loss = top + jnp.log(total) - chosen
    return (loss, query_embed)


def solution(mesh):
    return jax.shard_map(
        per_device,
        mesh=mesh,
        in_specs=(P("dp", "mp"), P("dp", "mp"), P("dp"), P("mp", None)),
        out_specs=(P("dp"), P("dp", None)),
        check_vma=False,
    )
```

profile of v0, /device:TPU:1, one launch (start us, length us, event | category | flops | bytes accessed | tf_op | source)
XLA Modules:
  0.0 118.8 jit_solution(1557416671414727782)
XLA Ops:
  0.6 1.2 %copy-done = bf16[512,1024]{1,0:T(8,128)(2,1)S(1)} copy-done((bf16[512,1024]{1,0:T(8,128)(2,1)S(1)}, bf16[512,1024]{1,0:T(8,128)(2,1)}, u32[]{:S(2)}) %copy-start) | copy-done | bytes 1048600
  1.9 2.0 %convolution_convert_fusion = bf16[512,128]{1,0:T(8,128)(2,1)} fusion(bf16[512,1024]{1,0:T(8,128)(2,1)S(1)} %copy-done, bf16[1024,128]{1,0:T(8,128)(2,1)} %param.9), kind=kOutput, calls=%fused_computation.28 | convolution fusion | flops 134283264 | bytes 1441792 | tf_op jit(solution)/shard_map/dot_general | solution.py:87
  3.9 4.8 %all-to-all-start = ((bf16[4,128,128]{2,1,0:T(8,128)(2,1)}), bf16[4,128,128]{2,1,0:T(8,128)(2,1)S(1)}, u32[]{:S(2)}, u32[]{:S(2)}) async-start(bf16[4,128,128]{2,1,0:T(8,128)(2,1)} %bitcast), calls=%async_computation | async-start | bytes 262144 | tf_op jit(solution)/shard_map/all_to_all | solution.py:26
  8.7 1.7 %fusion.21 = f32[512,128]{1,0:T(8,128)S(1)} fusion(bf16[512,1024]{1,0:T(8,128)(2,1)} %param.6, bf16[1024,128]{1,0:T(8,128)(2,1)} %param.9), kind=kOutput, calls=%fused_computation.44 | convolution fusion | flops 134217728 | bytes 1572864 | tf_op jit(solution)/shard_map/dot_general | solution.py:86
  10.4 3.1 %all-to-all-done = bf16[4,128,128]{2,1,0:T(8,128)(2,1)S(1)} async-done(((bf16[4,128,128]{2,1,0:T(8,128)(2,1)}), bf16[4,128,128]{2,1,0:T(8,128)(2,1)S(1)}, u32[]{:S(2)}, u32[]{:S(2)}) %all-to-all-start) | async-done | bytes 131104 | tf_op jit(solution)/shard_map/all_to_all | solution.py:26
  13.6 1.0 broadcast_in_dim.20
  14.6 3.5 %all-to-all-start.2 = ((f32[4,512,128]{2,1,0:T(8,128)}), f32[4,512,128]{2,1,0:T(8,128)S(1)}, u32[]{:S(2)}, u32[]{:S(2)}) async-start(f32[4,512,128]{2,1,0:T(8,128)} %broadcast_in_dim.20), calls=%async_computation.2 | async-start | bytes 2097152 | tf_op jit(solution)/shard_map/all_to_all | solution.py:9
  18.2 12.0 %all-to-all-done.2 = f32[4,512,128]{2,1,0:T(8,128)S(1)} async-done(((f32[4,512,128]{2,1,0:T(8,128)}), f32[4,512,128]{2,1,0:T(8,128)S(1)}, u32[]{:S(2)}, u32[]{:S(2)}) %all-to-all-start.2) | async-done | bytes 1048608 | tf_op jit(solution)/shard_map/all_to_all | solution.py:9
  30.2 1.8 %broadcast_in_dim.19 = bf16[64,128,128]{2,1,0:T(8,128)(2,1)} broadcast(bf16[128,128]{1,0:T(8,128)(2,1)S(1)} %reduce_sum.45), dimensions={1,2} | broadcast | bytes 2129920 | tf_op jit(solution)/shard_map/broadcast_in_dim | solution.py:10
  32.0 15.6 %all-to-all-start.1 = ((bf16[64,128,128]{2,1,0:T(8,128)(2,1)}), bf16[64,128,128]{2,1,0:T(8,128)(2,1)S(1)}, u32[]{:S(2)}, u32[]{:S(2)}) async-start(bf16[64,128,128]{2,1,0:T(8,128)(2,1)} %broadcast_in_dim.19), calls=%async_computation.1 | async-start | bytes 4194304 | tf_op jit(solution)/shard_map/all_to_all | solution.py:9
  47.7 1.3 %reduce_sum.46 = bf16[512,128]{1,0:T(8,128)(2,1)S(1)} reduce(f32[4,512,128]{2,1,0:T(8,128)} %copy-done.2, f32[]{:T(128)} %constant.81.clone.1), dimensions={0}, to_apply=%region_1.0 | reduce | flops 196608 | bytes 1179652 | tf_op jit(solution)/shard_map/reduce_sum | solution.py:16
  49.0 49.9 %all-to-all-done.1 = bf16[64,128,128]{2,1,0:T(8,128)(2,1)S(1)} async-done(((bf16[64,128,128]{2,1,0:T(8,128)(2,1)}), bf16[64,128,128]{2,1,0:T(8,128)(2,1)S(1)}, u32[]{:S(2)}, u32[]{:S(2)}) %all-to-all-start.1) | async-done | bytes 2097184 | tf_op jit(solution)/shard_map/all_to_all | solution.py:9
  98.9 12.4 %while.17 = (s32[]{:T(128)}, f32[512]{0:T(512)S(1)}, f32[512]{0:T(512)S(1)}, f32[512]{0:T(512)S(1)}, bf16[4,2048,128]{2,1,0:T(8,128)(2,1)S(1)}, /*index=5*/bf16[...) while((s32[]{:T(128)}, f32[512]{0:T(512)S(1)}, ...), condition=%wide.region_6.7_spmd.clone, body=%wide.region_2.6_spmd.clone.sunk | while | flops 274777600 | bytes 9089167 | solution.py:120
  98.9 0.7 fusion.33
  100.9 1.0 fusion.35
  101.9 0.7 fusion.33
  102.7 0.7 dynamic_slice.25
  104.0 1.0 fusion.35
  105.0 0.7 fusion.33
  105.8 0.7 dynamic_slice.25
  107.1 1.0 fusion.35
  108.1 0.7 fusion.33
  110.2 1.0 fusion.35
  111.3 6.7 %all_to_all.20 = f32[4,3,512]{2,1,0:T(4,128)S(1)} all-to-all(f32[4,3,512]{2,1,0:T(4,128)S(1)} %broadcast_in_dim.34), channel_id=1, replica_groups=mesh['dp'=64,'mp'=4] {'mp'}, dimensions={0} | all-to-all | bytes 49152 | tf_op jit(solution)/shard_map/all_to_all | solution.py:9
  (36 shorter events, 4.9 us)
Async XLA Ops:
  0.6 1.2 %copy-start = (bf16[512,1024]{1,0:T(8,128)(2,1)S(1)}, bf16[512,1024]{1,0:T(8,128)(2,1)}, u32[]{:S(2)}) copy-start(bf16[512,1024]{1,0:T(8,128)(2,1)} %param.7) | copy-start | bytes 3145732
  3.9 9.7 %all-to-all-start = ((bf16[4,128,128]{2,1,0:T(8,128)(2,1)}), bf16[4,128,128]{2,1,0:T(8,128)(2,1)S(1)}, u32[]{:S(2)}, u32[]{:S(2)}) async-start(bf16[4,128,128]{2,1,0:T(8,128)(2,1)} %bitcast), calls=%async_computation | async-start | bytes 262144 | tf_op jit(solution)/shard_map/all_to_all | solution.py:26
  14.6 15.6 %all-to-all-start.2 = ((f32[4,512,128]{2,1,0:T(8,128)}), f32[4,512,128]{2,1,0:T(8,128)S(1)}, u32[]{:S(2)}, u32[]{:S(2)}) async-start(f32[4,512,128]{2,1,0:T(8,128)} %broadcast_in_dim.20), calls=%async_computation.2 | async-start | bytes 2097152 | tf_op jit(solution)/shard_map/all_to_all | solution.py:9
  18.1 80.7 %copy-start.3 = (s32[512]{0:T(512)S(1)}, s32[512]{0:T(512)}, u32[]{:S(2)}) copy-start(s32[512]{0:T(512)} %param.8) | copy-start | bytes 6148
  30.2 1.8 %copy-start.2 = (f32[4,512,128]{2,1,0:T(8,128)}, f32[4,512,128]{2,1,0:T(8,128)S(1)}, u32[]{:S(2)}) copy-start(f32[4,512,128]{2,1,0:T(8,128)S(1)} %all-to-all-done.2) | copy-start | bytes 3145732
  32.0 66.8 %all-to-all-start.1 = ((bf16[64,128,128]{2,1,0:T(8,128)(2,1)}), bf16[64,128,128]{2,1,0:T(8,128)(2,1)S(1)}, u32[]{:S(2)}, u32[]{:S(2)}) async-start(bf16[64,128,128]{2,1,0:T(8,128)(2,1)} %broadcast_in_dim.19), calls=%async_computation.1 | async-start | bytes 4194304 | tf_op jit(solution)/shard_map/all_to_all | solution.py:9
  111.2 7.5 %copy-start.1 = (bf16[512,128]{1,0:T(8,128)(2,1)}, bf16[512,128]{1,0:T(8,128)(2,1)S(1)}, u32[]{:S(2)}) copy-start(bf16[512,128]{1,0:T(8,128)(2,1)S(1)} %get-tuple-element.290) | copy-start | bytes 393220
where the time goes:
time: 119 us
  waiting for transfers between devices  65 us (55%)
  starting transfers between devices  24 us (20%)
  other arithmetic  8.73 us (7%)
  local copies, waits for them, and re-layouts  6.93 us (6%)
  blocking collectives  6.65 us (6%)
  matrix products  6.62 us (6%)
    all_to_all x2, waiting for transfers between devices, copy_for_each(): lax.all_to_all(jnp.broadcast_to(array[None], (devices, *array.shape)), ax...  61.9 us
    all_to_all x2, starting transfers between devices, copy_for_each(): lax.all_to_all(jnp.broadcast_to(array[None], (devices, *array.shape)), ax...  19.1 us
    all_to_all x1, blocking collectives, copy_for_each(): lax.all_to_all(jnp.broadcast_to(array[None], (devices, *array.shape)), ax...  6.65 us
    all_to_all x1, starting transfers between devices, summed_on_arrival(): lax.all_to_all(cut_along(array, dim, devices), axis, 0, 0, tiled=True)  4.83 us
    reduce_sum x4, other arithmetic, step(): chosen = jnp.sum(jnp.where(hit, scores, 0.0), axis=1)  4.1 us
    all_to_all x1, waiting for transfers between devices, summed_on_arrival(): lax.all_to_all(cut_along(array, dim, devices), axis, 0, 0, tiled=True)  3.13 us
    broadcast_in_dim x3, local copies, waits for them, and re-layouts, copy_for_each(): jnp.broadcast_to(array[None], (devices, *array.shape))  2.89 us
    dot_general x4, matrix products, step(): lax.dot_general(query_embed, block, (((1,), (1,)), ((), ())), preferred_e...  2.88 us
  transfers between devices with their start and end apart: 3, of which 3 were waited for; matrix products, arithmetic and copies ran while one was open for 3% of the time, Pallas kernels for 0%

commit v1 on v0

v1 whole, which is shorter than its diff:
```python
import functools

import jax
import jax.numpy as jnp
from jax import lax
from jax.experimental import pallas as pl
from jax.experimental.pallas import tpu as pltpu
from jax.sharding import PartitionSpec as P

MESH = pl.DeviceIdType.MESH
X, Y, Z = 4, 4, 8
F32 = jnp.float32
BF16 = jnp.bfloat16


def signed_step(slot):
    return ((slot + 1) // 2) * (2 * (slot % 2) - 1)


def slot_of(step, size):
    if step == 0:
        return 0
    return 2 * step - 1 if step <= size // 2 else 2 * (size - step)


def kernel(
    queries,
    passages,
    labels,
    projection,
    loss_out,
    embed_out,
    weights,
    raw,
    part_send,
    part_recv,
    pas,
    qry,
    lab,
    target,
    top,
    total,
    chosen,
    stat_send,
    stat_recv,
    load_sem,
    store_sem,
    rs_send,
    rs_recv,
    lab_send,
    lab_recv,
    pz_send,
    pz_recv,
    pc_send,
    pc_recv,
    qa_send,
    qa_recv,
    qb_send,
    qb_recv,
    st_send,
    st_recv,
):
    dp = lax.axis_index("dp")
    x = lax.axis_index("mp")
    c = dp % 2
    z = (dp // 2) % Z
    y = dp // (2 * Z)
    share = raw.shape[2]

    def at(dx=0, dy=0, dz=0, other=False):
        core = 1 - c if other else c
        return ((((y + dy) % Y) * Z + (z + dz) % Z) * 2 + core, (x + dx) % X)

    def remote(src, dst, send, recv, device):
        return pltpu.make_async_remote_copy(
            src_ref=src,
            dst_ref=dst,
            send_sem=send,
            recv_sem=recv,
            device_id=device,
            device_id_type=MESH,
        )

    started = []

    def send(*args):
        copy = remote(*args)
        copy.start()
        started.append(copy)

    def arrived(dst, recv):
        remote(dst, dst, recv, recv, at(dx=1)).wait_recv()

    loads = {}
    first = pltpu.make_async_copy(projection, weights, load_sem.at[0])
    first.start()
    order = (2, 1, 3, 0)
    for tower, states in enumerate((passages, queries)):
        for r in order:
            rows = pl.ds(((x + r) % X) * share, share)
            copy = pltpu.make_async_copy(
                states.at[rows], raw.at[tower, r], load_sem.at[1 + tower * X + r]
            )
            copy.start()
            loads[tower, r] = copy

    peers = [at(dx=dx, dy=dy) for dx in range(X) for dy in range(Y) if dx or dy]
    peers += [at(dz=dz) for dz in range(1, Z)] + [at(other=True)]
    barrier = pltpu.get_barrier_semaphore()
    for peer in peers:
        pl.semaphore_signal(barrier, inc=1, device_id=peer, device_id_type=MESH)

    first.wait()

    def partial(tower, r):
        loads[tower, r].wait()
        return jnp.dot(raw[tower, r], weights[...], preferred_element_type=F32)

    for tower in range(2):
        for r in order[:-1]:
            part_send[tower, r] = partial(tower, r).astype(BF16)
        if tower == 0:
            pl.semaphore_wait(barrier, len(peers))
        for r in order[:-1]:
            send(
                part_send.at[tower, r],
                part_recv.at[tower, r],
                rs_send.at[tower, r],
                rs_recv.at[tower, r],
                at(dx=r),
            )
    for r in range(1, Y):
        send(labels, lab.at[slot_of(r, Y)], lab_send.at[r], lab_recv.at[r], at(dy=r))
    lab[0] = labels[...]
    own = [partial(tower, 0) for tower in range(2)]

    def summed(tower):
        value = own[tower]
        for r in (1, 3, 2):
            arrived(part_recv.at[tower, r], rs_recv.at[tower, r])
            value = value + part_recv[tower, r].astype(F32)
        return value.astype(BF16)

    pas[0, c] = summed(0)
    for r in (4, 3, 5, 2, 6, 1, 7):
        send(
            pas.at[0, c], pas.at[slot_of(r, Z), c], pz_send.at[r], pz_recv.at[r], at(dz=r)
        )
    send(pas.at[0, c], pas.at[0, c], pc_send.at[0], pc_recv.at[0], at(other=True))

    half = share // 2
    qry[0, x] = summed(1)

    def lines(slot, block, side):
        return qry.at[slot, block, pl.ds(side * half, half)]

    def forward_y(rx):
        block = (x - rx + X) % X
        for ry in (2, 1, 3):
            send(
                lines(0, block, 0),
                lines(slot_of(ry, Y), block, 0),
                qb_send.at[0, rx, ry],
                qb_recv.at[0, rx, ry],
                at(dy=ry),
            )

    def forward_x(ry):
        slot = slot_of(ry, Y)
        for rx in (2, 1, 3):
            send(
                lines(slot, x, 1),
                lines(slot, x, 1),
                qb_send.at[1, ry, rx],
                qb_recv.at[1, ry, rx],
                at(dx=rx),
            )

    for r in (2, 1, 3):
        send(lines(0, x, 0), lines(0, x, 0), qa_send.at[0, r], qa_recv.at[0, r], at(dx=r))
        send(
            lines(0, x, 1),
            lines(slot_of(r, Y), x, 1),
            qa_send.at[1, r],
            qa_recv.at[1, r],
            at(dy=r),
        )
    forward_y(0)
    forward_x(0)

    def relay_query(r):
        arrived(lines(0, (x - r + X) % X, 0), qa_recv.at[0, r])
        forward_y(r)
        arrived(lines(slot_of(r, Y), x, 1), qa_recv.at[1, r])
        forward_x(r)

    def relay_passage(r):
        slot = slot_of(r, Z)
        arrived(pas.at[slot, c], pz_recv.at[r])
        send(pas.at[slot, c], pas.at[slot, c], pc_send.at[r], pc_recv.at[r], at(other=True))

    def passage_here(r):
        arrived(pas.at[slot_of(r, Z), 1 - c], pc_recv.at[r])

    def queries_here(ry):
        slot = slot_of(ry, Y)
        for rx in range(X):
            block = (x - rx + X) % X
            if ry:
                arrived(lines(slot, block, 0), qb_recv.at[0, rx, ry])
            if rx:
                arrived(lines(slot, block, 1), qb_recv.at[1, ry, rx])
        if ry:
            arrived(lab.at[slot], lab_recv.at[ry])
        sub = lax.broadcasted_iota(jnp.int32, (8, share), 0)
        for block in range(X):
            where = pl.ds(block * share, share)
            line = lab[slot, pl.ds(block, 1), :]
            target[slot, :, where] = line - (y * Z * 2 * X + x) * share - sub
        top[slot] = jnp.full(top.shape[1:], -jnp.inf, F32)
        total[slot] = jnp.zeros(total.shape[1:], F32)
        chosen[slot] = jnp.zeros(chosen.shape[1:], F32)

    width = 2 * share

    def tile(group, slot):
        source = (z - signed_step(slot) + Z) % Z
        rows = pas[slot].reshape(2 * share, share)
        for part in range(X * share // width):
            cols = pl.ds(part * width, width)
            block = qry[group, pl.ds(2 * part, 2)].reshape(width, share)
            scores = lax.dot_general(
                rows, block, (((1,), (1,)), ((), ())), preferred_element_type=F32
            )
            aim = target[group, :, cols] - source * (2 * X * share)
            pick = chosen[group, :, cols]
            high = top[group, :, cols]
            before = high
            for k in range(2 * share // 8):
                line = scores[8 * k : 8 * k + 8]
                index = (8 * k // share) * X * share + 8 * k % share
                pick = jnp.where(aim == index, line, pick)
                high = jnp.maximum(high, line)
            chosen[group, :, cols] = pick
            top[group, :, cols] = high
            mass = total[group, :, cols] * jnp.exp(before - high)
            for k in range(2 * share // 8):
                mass = mass + jnp.exp(scores[8 * k : 8 * k + 8] - high)
            total[group, :, cols] = mass

    def tiles(group, low, high):
        def body(slot, carry):
            tile(group, slot)
            return carry

        lax.fori_loop(low, high, body, 0)

    def finish(group, ry):
        peak = jnp.max(top[group], axis=0, keepdims=True)
        mass = jnp.sum(total[group] * jnp.exp(top[group] - peak), axis=0, keepdims=True)
        lse = peak + jnp.log(mass)
        hit = jnp.sum(chosen[group], axis=0, keepdims=True)
        into = stat_recv if group == 0 else stat_send
        for place in (stat_send, stat_recv) if group == 0 else (stat_send,):
            for block in range(X):
                cut = slice(block * share, (block + 1) * share)
                place[group, pl.ds(block, 1), :] = lse[:, cut]
                place[group, pl.ds(X + block, 1), :] = hit[:, cut]
        for rx in (2, 1, 3, 0):
            if rx or ry:
                send(
                    stat_send.at[group],
                    stat_recv.at[rx * Y + group],
                    st_send.at[rx, group],
                    st_recv.at[rx, group],
                    at(dx=rx, dy=(Y - ry) % Y),
                )

    relay_query(1)
    relay_query(3)
    relay_passage(1)
    relay_passage(7)
    relay_query(2)
    relay_passage(2)
    relay_passage(6)
    passage_here(0)
    passage_here(1)
    passage_here(7)
    queries_here(0)
    stores = []
    for block in range(X):
        copy = pltpu.make_async_copy(
            qry.at[0, block], embed_out.at[pl.ds(block * share, share)], store_sem.at[block]
        )
        copy.start()
        stores.append(copy)
    tiles(0, 0, 3)
    relay_passage(3)
    relay_passage(5)
    passage_here(2)
    passage_here(6)
    tiles(0, 3, 5)
    queries_here(1)
    tiles(1, 0, 5)
    relay_passage(4)
    queries_here(3)
    tiles(2, 0, 5)
    passage_here(3)
    passage_here(5)
    for group in range(3):
        tiles(group, 5, 7)
    queries_here(2)
    passage_here(4)
    tiles(3, 0, 8)
    finish(3, 2)
    tiles(1, 7, 8)
    finish(1, 1)
    tiles(2, 7, 8)
    finish(2, 3)
    tiles(0, 7, 8)
    finish(0, 0)

    for rx in range(X):
        for group in range(Y):
            if rx or group:
                arrived(stat_recv.at[rx * Y + group], st_recv.at[rx, group])
    parts = stat_recv[...]
    lse, hit = parts[:, :X], parts[:, X:]
    peak = jnp.max(lse, axis=0)
    mass = jnp.sum(jnp.exp(lse - peak[None]), axis=0)
    loss_out[...] = peak + jnp.log(mass) - jnp.sum(hit, axis=0)

    for copy in stores:
        copy.wait()
    for copy in started:
        copy.wait_send()


def per_device(queries, passages, labels, projection):
    rows, depth = queries.shape
    embed = projection.shape[1]
    share = rows // X
    dma = pltpu.SemaphoreType.DMA
    vmem = pl.BlockSpec(memory_space=pltpu.VMEM)
    hbm = pl.BlockSpec(memory_space=pl.ANY)
    loss, query_embed = pl.pallas_call(
        kernel,
        out_shape=(
            jax.ShapeDtypeStruct((X, share), F32),
            jax.ShapeDtypeStruct((rows, embed), BF16),
        ),
        in_specs=[hbm, hbm, vmem, hbm],
        out_specs=(vmem, hbm),
        scratch_shapes=[
            pltpu.VMEM((depth, embed), BF16),
            pltpu.VMEM((2, X, share, depth), BF16),
            pltpu.VMEM((2, X, share, embed), BF16),
            pltpu.VMEM((2, X, share, embed), BF16),
            pltpu.VMEM((Z, 2, share, embed), BF16),
            pltpu.VMEM((Y, X, share, embed), BF16),
            pltpu.VMEM((Y, X, share), jnp.int32),
            pltpu.VMEM((Y, 8, rows), jnp.int32),
            pltpu.VMEM((Y, 8, rows), F32),
            pltpu.VMEM((Y, 8, rows), F32),
            pltpu.VMEM((Y, 8, rows), F32),
            pltpu.VMEM((Y, 2 * X, share), F32),
            pltpu.VMEM((X * Y, 2 * X, share), F32),
            dma((1 + 2 * X,)),
            dma((X,)),
            dma((2, X)),
            dma((2, X)),
            dma((Y,)),
            dma((Y,)),
            dma((Z,)),
            dma((Z,)),
            dma((Z,)),
            dma((Z,)),
            dma((2, X)),
            dma((2, X)),
            dma((2, X, Y)),
            dma((2, X, Y)),
            dma((X, Y)),
            dma((X, Y)),
        ],
        compiler_params=pltpu.CompilerParams(
            collective_id=0, has_side_effects=True, vmem_limit_bytes=67_000_000
        ),
    )(queries, passages, labels.reshape(X, share), projection)
    return loss.reshape(rows), query_embed


def solution(mesh):
    return jax.shard_map(
        per_device,
        mesh=mesh,
        in_specs=(P("dp", "mp"), P("dp", "mp"), P("dp"), P("mp", None)),
        out_specs=(P("dp"), P("dp", None)),
        check_vma=False,
    )
```

time: 119 us -> 42.9 us (0.36)
  waiting for transfers between devices: 65 us -> 0 us
  Pallas kernels: 0 us -> 39.3 us
  starting transfers between devices: 24 us -> 0 us
  other arithmetic: 8.73 us -> 0 us
  blocking collectives: 6.65 us -> 0 us
  matrix products: 6.62 us -> 0 us
  local copies, waits for them, and re-layouts: 6.93 us -> 2.79 us
    all_to_all x3 -> x0, waiting for transfers between devices: 65 us -> none  [the longest x2 61.9 us: copy_for_each(): lax.all_to_all(jnp.broadcast_to(array[None], (devices, *array.shape)), ax...]
    pallas_call x0 -> x1, Pallas kernels: none -> 39.3 us  [per_device(): pl.pallas_call(kernel, out_shape=(jax.ShapeDtypeStruct((X, share), F32),...]
    all_to_all x3 -> x0, starting transfers between devices: 24 us -> none  [the longest x2 19.1 us: copy_for_each(): lax.all_to_all(jnp.broadcast_to(array[None], (devices, *array.shape)), ax...]
    all_to_all x1 -> x0, blocking collectives: 6.65 us -> none  [copy_for_each(): lax.all_to_all(jnp.broadcast_to(array[None], (devices, *array.shape)), ax...]
    dot_general x6 -> x0, matrix products: 6.62 us -> none  [the longest x4 2.88 us: step(): lax.dot_general(query_embed, block, (((1,), (1,)), ((), ())), preferred_e...]
    reduce_sum x6 -> x0, other arithmetic: 5.41 us -> none  [the longest x4 4.1 us: step(): chosen = jnp.sum(jnp.where(hit, scores, 0.0), axis=1)]
    broadcast_in_dim x3 -> x0, local copies, waits for them, and re-layouts: 2.89 us -> none  [copy_for_each(): jnp.broadcast_to(array[None], (devices, *array.shape))]
    add x10 -> x0, other arithmetic: 2.7 us -> none  [the longest x4 2.58 us: step(): passage_ids = columns // width * rows + offset + columns % width]
  transfers between devices with their start and end apart: 3 -> 0, of which waited for: 3 -> 0; matrix products, arithmetic and copies ran while one was open for 3% -> 0% of each run, Pallas kernels for 0% -> 0%
where the time goes in v1:
time: 42.9 us; the launch traced here: 42.7 us
  Pallas kernels  39.3 us (92%)
  local copies, waits for them, and re-layouts  2.79 us (7%)
  between operations  0.65 us (2%)
    pallas_call x1, Pallas kernels, per_device(): pl.pallas_call(kernel, out_shape=(jax.ShapeDtypeStruct((X, share), F32),...  39.3 us
    unnamed x4, local copies, waits for them, and re-layouts  2.79 us

profile of v1, /device:TPU:1, one launch (start us, length us, event | category | flops | bytes accessed | tf_op | source)
XLA Modules:
  0.0 42.7 jit_solution(11719403101813376635)
XLA Ops:
  0.6 39.3 %shard_map.59 = (f32[4,128]{1,0:T(4,128)}, bf16[512,128]{1,0:T(8,128)(2,1)}) custom-call(bf16[512,1024]{1,0:T(8,128)(2,1)} %queries.1, bf16[512,1024]{1,0:T(8,128)(2,1)} %passages.1, s32[4,128]{1,0:T(4,128)} %bitcast.3, bf16[1024,128]{1,0:T(8,128)(2,1)} %projection.1), custom_call_target="tpu_custom_call" | custom-call | tf_op jit(solution)/shard_map/pallas_call | solution.py:346
  39.9 0.0 copy-start
  39.9 0.6 %copy-done = f32[4,128]{1,0:T(4,128)S(1)} copy-done((f32[4,128]{1,0:T(4,128)S(1)}, f32[4,128]{1,0:T(4,128)}, u32[]{:S(2)}) %copy-start) | copy-done | bytes 2072
  40.6 0.6 %copy.8 = f32[512]{0:T(512)} copy(f32[512]{0:T(512)S(1)} %bitcast.2) | data formatting | bytes 4096
  41.2 1.6 %copy.9 = bf16[512,128]{1,0:T(8,128)(2,1)} copy(bf16[512,128]{1,0:T(8,128)(2,1)} %get-tuple-element.9) | data formatting | bytes 262144
Async XLA Ops:
  39.9 0.7 %copy-start = (f32[4,128]{1,0:T(4,128)S(1)}, f32[4,128]{1,0:T(4,128)}, u32[]{:S(2)}) copy-start(f32[4,128]{1,0:T(4,128)} %get-tuple-element.4) | copy-start | bytes 6148
